TPU v7x, 32 devices: a whole 2x2x4 slice. The times are simulated.
32 devices in a mesh: blk: 16 (over z, y, x), grp: 2 (over core).
Axes of the slice: x: 2, y: 2, z: 4, core: 2. Of those that a mesh axis runs over, the one named last changes fastest.
Arguments:
- sky_maps: float32 [4, 128, 4096], P(None, ('blk', 'grp')), may hold values from -6 to 6
- legendre: bfloat16 [128, 512, 2048], P(('blk', 'grp')), may hold values from -0.5 to 0.5
- owner_table: int32 [512], replicated, may hold values from 0 to 511, each once
Outputs:
- harmonics: float32 [512, 4, 2, 2048], P(('blk', 'grp'))
- spectra: float32 [10, 2048], P(None, ('blk', 'grp'))
Inputs may be any that keep to these rules, and one draw needn't show every extreme that they name: `owner_table`: a permutation of the orders 0 to 511.
All inputs are finite; a program needn't handle non-finite values.
Results may differ from a plain program's by a relative error of at most 0.0034.
Values may be sent and summed in bfloat16 or wider, within the bound.
A program may use at most 128 MiB of HBM per device.

v0:
```python
import math
import jax
import jax.numpy as jnp
import numpy as np
from jax import lax
from jax.sharding import PartitionSpec as P


def cycle_fourier(sky_maps, order_count):
    map_count, cycle_count, pixels = sky_maps.shape
    pixel_index = lax.iota(jnp.int32, pixels)
    order_index = lax.iota(jnp.int32, order_count)
    phase = (pixel_index[:, None] * order_index[None, :] % pixels).astype(jnp.float32) * (
        2.0 * math.pi / pixels
    )
    table = jnp.concatenate([jnp.cos(phase), -jnp.sin(phase)], axis=1) / math.sqrt(pixels)
    flat = sky_maps.reshape(map_count * cycle_count, pixels)
    spectral = jnp.dot(
        flat, table, precision=lax.Precision.HIGHEST, preferred_element_type=jnp.float32
    )
    spectral = spectral.reshape(map_count, cycle_count, 2, order_count)
    spectral = jnp.transpose(spectral, (1, 0, 2, 3)).reshape(
        cycle_count, 2 * map_count, order_count
    )
    return spectral.astype(jnp.bfloat16)


def per_device(sky_maps, legendre, owner_table):
    map_count = sky_maps.shape[0]
    order_count = legendre.shape[1]
    ell_count = legendre.shape[2]
    devices_all = lax.axis_size(("blk", "grp"))
    own_count = order_count // devices_all
    my_index = lax.axis_index(("blk", "grp"))
    owned_orders = lax.dynamic_slice_in_dim(owner_table, my_index * own_count, own_count)
    fourier = cycle_fourier(sky_maps, order_count)
    table_perm = jnp.take(legendre, owner_table, axis=1)
    fourier_perm = jnp.take(fourier, owner_table, axis=2)
    four_cols = jnp.transpose(fourier_perm, (0, 2, 1))
    table_own, four_own = (
        lax.all_to_all(table_perm, ("blk", "grp"), split_axis=1, concat_axis=0, tiled=True),
        lax.all_to_all(four_cols, ("blk", "grp"), split_axis=1, concat_axis=0, tiled=True),
    )
    summed = jnp.einsum("rmc,rml->mcl", four_own, table_own, preferred_element_type=jnp.float32)
    ell_index = lax.iota(jnp.int32, ell_count)
    keep = ell_index[None, None, :] >= owned_orders[:, None, None]
    summed = jnp.where(keep, summed, jnp.zeros_like(summed))
    harmonics = summed.reshape(own_count, map_count, 2, ell_count)
    weight = jnp.where(owned_orders == 0, 1.0, 2.0).astype(jnp.float32)
    cross = jnp.einsum("m,miql,mjql->ijl", weight, harmonics, harmonics)
    first_map, second_map = np.triu_indices(map_count)
    pair_terms = cross[first_map, second_map]
    ell_share = ell_count // devices_all
    owned_power = lax.psum_scatter(pair_terms, ("blk", "grp"), scatter_dimension=1, tiled=True)
    owned_ells = my_index * ell_share + lax.iota(jnp.int32, ell_share)
    spectra = owned_power / (2 * owned_ells + 1).astype(jnp.float32)[None, :]
    return (harmonics, spectra)


def solution(mesh):
    return jax.shard_map(
        per_device,
        mesh=mesh,
        in_specs=(P(None, ("blk", "grp"), None), P(("blk", "grp"), None, None), P()),
        out_specs=(P(("blk", "grp"), None, None, None), P(None, ("blk", "grp"))),
        check_vma=False,
    )
```

profile of v0, /device:TPU:0, one launch (start us, length us, event | category | flops | bytes accessed | tf_op | source)
XLA Modules:
  0.0 506.8 jit_solution(16573717867274145722)
XLA Ops:
  7.2 0.0 copy-start.3
  7.2 0.0 copy-start.1
  7.2 34.6 %sine_negate_fusion = (f32[4096,512]{1,0:T(8,128)}, f32[4096,512]{1,0:T(8,128)}) fusion(), kind=kLoop, calls=%fused_computation.16 | loop fusion | flops 31457280 | bytes 16777216 | tf_op jit(solution)/shard_map/neg | solution.py:16
  41.8 0.0 copy-done.3
  41.8 0.0 copy-done.1
  41.9 0.1 reshape.47
  42.0 12.7 %fusion.12 = bf16[16,1024]{1,0:T(8,128)(2,1)S(1)} fusion(f32[16,4096]{1,0:T(8,128)S(1)} %reshape.47, f32[4096,512]{1,0:T(8,128)} %get-tuple-element.4, f32[4096,512]{1,0:T(8,128)} %get-tuple-element.5), kind=kOutput, calls=%fused_computation.24 | convolution fusion | flops 813711360 | bytes 17072128 | tf_op jit(solution)/shard_map/dot_general | solution.py:18
  54.7 0.3 copy.23
  55.0 2.1 gather_fusion
  57.1 1.8 fusion.15
  58.9 1.2 reshape.76
  60.0 7.3 %all-to-all-start = ((bf16[32,2,256]{2,1,0:T(2,128)(2,1)}), bf16[32,2,256]{2,1,0:T(2,128)(2,1)S(1)}, u32[]{:S(2)}, u32[]{:S(2)}) async-start(bf16[32,2,256]{2,1,0:T(2,128)(2,1)} %reshape.76), calls=%async_computation | async-start | bytes 65536 | tf_op jit(solution)/shard_map/all_to_all | solution.py:42
  67.4 35.2 %gather_fusion.1 = bf16[512,4,2048]{2,0,1:T(8,128)(2,1)} fusion(bf16[4,512,2048]{2,1,0:T(8,128)(2,1)} %param.8, s32[1024]{0:T(1024)S(1)} %pad_clamp_fusion), kind=kCustom, calls=%fused_computation.1 | custom fusion | bytes 16779264 | tf_op jit(solution)/shard_map/jit(_take)/gather | solution.py:37
  102.5 7.6 %select_bitcast_fusion = bf16[4,512,2048]{2,1,0:T(8,128)(2,1)} fusion(bf16[512,4,2048]{2,0,1:T(8,128)(2,1)} %gather_fusion.1, pred[512]{0:T(512)(128)(4,1)S(1)} %compare_and_fusion), kind=kLoop, calls=%fused_computation.14 | loop fusion | flops 4194304 | bytes 16777728 | tf_op jit(solution)/shard_map/jit(_take)/select_n | solution.py:37
  110.1 12.1 %copy.26 = bf16[4,512,2048]{2,0,1:T(4,128)(2,1)} copy(bf16[4,512,2048]{2,1,0:T(8,128)(2,1)} %select_bitcast_fusion) | data formatting | bytes 16777216 | tf_op jit(solution)/shard_map/jit(_take)/select_n | solution.py:37
  122.2 0.0 all-to-all-done
  122.2 6.0 %all-to-all-start.1 = ((bf16[4,512,2048]{2,0,1:T(4,128)(2,1)}), bf16[4,512,2048]{2,0,1:T(4,128)(2,1)}, u32[]{:S(2)}, u32[]{:S(2)}) async-start(bf16[4,512,2048]{2,0,1:T(4,128)(2,1)} %copy.26), calls=%async_computation.1 | async-start | bytes 16777216 | tf_op jit(solution)/shard_map/all_to_all | solution.py:41
  128.2 0.0 reduce-scatter.4.cloned.1.call-start
  128.3 0.1 compare_select_fusion.1
  128.3 0.1 iota_compare_fusion
  128.4 0.6 reshape.77
  129.1 0.3 copy.34
  129.4 0.2 copy.28
  129.6 184.5 %all-to-all-done.1 = bf16[4,512,2048]{2,0,1:T(4,128)(2,1)} async-done(((bf16[4,512,2048]{2,0,1:T(4,128)(2,1)}), bf16[4,512,2048]{2,0,1:T(4,128)(2,1)}, u32[]{:S(2)}, u32[]{:S(2)}) %all-to-all-start.1) | async-done | bytes 8388640 | tf_op jit(solution)/shard_map/all_to_all | solution.py:41
  314.1 8.5 %copy.38 = bf16[4,32,16,2048]{3,0,1,2:T(4,128)(2,1)} copy(bf16[4,32,16,2048]{3,0,2,1:T(4,128)(2,1)} %bitcast.9) | data formatting | bytes 16777216 | tf_op jit(solution)/shard_map/all_to_all | solution.py:41
  322.6 12.6 %all_to_all.33 = bf16[128,16,2048]{2,0,1:T(8,128)(2,1)} reshape(bf16[32,4,16,2048]{3,1,0,2:T(4,128)(2,1)} %bitcast.37) | data formatting | bytes 16777216 | tf_op jit(solution)/shard_map/all_to_all | solution.py:41
  335.2 4.6 convolution_select_fusion
  339.8 0.6 reshape.48
  340.4 0.0 copy-start
  340.4 5.5 %copy.30 = bf16[16,4,2,2048]{0,1,2,3:T(4,128)(2,1)} copy(f32[16,4,2,2048]{3,2,1,0:T(2,128)S(1)} %reshape.48) | data formatting | bytes 1572864 | tf_op jit(solution)/shard_map/reshape | solution.py:48
  345.9 0.5 broadcast_multiply_fusion
  346.4 4.9 copy.29
  351.3 0.0 copy-start.2
  351.3 7.8 %convolution_bitcast_fusion = f32[4,4,2048]{1,0,2:T(4,128)} fusion(bf16[16,4,2,2048]{0,1,2,3:T(4,128)(2,1)} %copy.29, bf16[16,4,2,2048]{0,1,2,3:T(4,128)(2,1)} %copy.30), kind=kOutput, calls=%fused_computation.22 | convolution fusion | flops 2097152 | bytes 1179648 | tf_op jit(solution)/shard_map/m,miql,mjql->ijl/dot_general | solution.py:50
  359.1 0.0 copy-done
  359.1 3.6 copy.31
  362.6 0.0 copy-done.2
  362.6 0.8 gather_fusion.2
  363.4 1.3 copy.35
  364.8 0.0 reduce-scatter.4.cloned.1.call-update
  364.8 133.7 %reduce-scatter.4.cloned.1.call-done = f32[64,10]{1,0:T(8,128)} async-done(((f32[2048,10]{1,0:T(8,128)}), f32[64,10]{1,0:T(8,128)}) %reduce-scatter.4.cloned.1.call-update) | async-done | bytes 2576
  498.5 0.8 copy.36
  499.4 0.6 broadcast_divide_fusion
  (6 shorter events, 0.1 us)
Async XLA Ops:
  7.2 34.6 %copy-start.3 = (s32[512]{0:T(512)S(1)}, s32[512]{0:T(512)}, u32[]{:S(2)}) copy-start(s32[512]{0:T(512)} %param.9) | copy-start | bytes 6148
  7.2 34.7 %copy-start.1 = (f32[4,4,4096]{2,1,0:T(4,128)S(1)}, f32[4,4,4096]{2,1,0:T(4,128)}, u32[]{:S(2)}) copy-start(f32[4,4,4096]{2,1,0:T(4,128)} %param.7) | copy-start | bytes 786436
  60.0 62.2 %all-to-all-start = ((bf16[32,2,256]{2,1,0:T(2,128)(2,1)}), bf16[32,2,256]{2,1,0:T(2,128)(2,1)S(1)}, u32[]{:S(2)}, u32[]{:S(2)}) async-start(bf16[32,2,256]{2,1,0:T(2,128)(2,1)} %reshape.76), calls=%async_computation | async-start | bytes 65536 | tf_op jit(solution)/shard_map/all_to_all | solution.py:42
  122.2 191.9 %all-to-all-start.1 = ((bf16[4,512,2048]{2,0,1:T(4,128)(2,1)}), bf16[4,512,2048]{2,0,1:T(4,128)(2,1)}, u32[]{:S(2)}, u32[]{:S(2)}) async-start(bf16[4,512,2048]{2,0,1:T(4,128)(2,1)} %copy.26), calls=%async_computation.1 | async-start | bytes 16777216 | tf_op jit(solution)/shard_map/all_to_all | solution.py:41
  128.2 370.3 %reduce-scatter.4.cloned.1.call-start = ((), (), s32[]{:S(2)}) async-start(), calls=%async_computation.3 | async-start | bytes 1081344
  340.4 18.7 %copy-start = (f32[16,4,2,2048]{3,2,1,0:T(2,128)}, f32[16,4,2,2048]{3,2,1,0:T(2,128)S(1)}, u32[]{:S(2)}) copy-start(f32[16,4,2,2048]{3,2,1,0:T(2,128)S(1)} %reshape.48) | copy-start | bytes 3145732
  351.3 11.3 %copy-start.2 = (s32[10]{0:T(128)S(1)}, s32[10]{0:T(128)}, u32[]{:S(2)}) copy-start(s32[10]{0:T(128)} %constant.109) | copy-start | bytes 124
Sparse Core Ops, SparseCore 0:
  364.9 133.5 reduce-scatter.3
where the time goes:
time: 508 us; the launch traced here: 507 us
  waiting for transfers between devices  318 us (63%)
  local copies, waits for them, and re-layouts  90.7 us (18%)
  other arithmetic  45.3 us (9%)
  matrix products  25 us (5%)
  between operations  14.2 us (3%)
  starting transfers between devices  13.3 us (3%)
    all_to_all x1, waiting for transfers between devices, per_device(): lax.all_to_all(table_perm, ('blk', 'grp'), split_axis=1, concat_axis=0, t...  185 us
    unnamed x2, waiting for transfers between devices  134 us
    gather x1, local copies, waits for them, and re-layouts, per_device(): table_perm = jnp.take(legendre, owner_table, axis=1)  35.2 us
    neg x1, other arithmetic, cycle_fourier(): -jnp.sin(phase)  34.6 us
    all_to_all x2, local copies, waits for them, and re-layouts, per_device(): lax.all_to_all(table_perm, ('blk', 'grp'), split_axis=1, concat_axis=0, t...  21.1 us
    dot_general x1, matrix products, cycle_fourier(): jnp.dot(flat, table, precision=lax.Precision.HIGHEST, preferred_element_t...  12.7 us
    select_n x1, local copies, waits for them, and re-layouts, per_device(): table_perm = jnp.take(legendre, owner_table, axis=1)  12.1 us
  transfers between devices with their start and end apart: 3, of which 2 were waited for; matrix products, arithmetic and copies ran while one was open for 11% of the time, Pallas kernels for 0%

commit v1 on v0

--- a/solution.py
+++ b/solution.py
@@ -38,7 +38,15 @@
     fourier_perm = jnp.take(fourier, owner_table, axis=2)
     four_cols = jnp.transpose(fourier_perm, (0, 2, 1))
     table_own, four_own = (
-        lax.all_to_all(table_perm, ("blk", "grp"), split_axis=1, concat_axis=0, tiled=True),
+        jnp.concatenate(
+            lax.all_to_all(
+                jnp.stack(jnp.split(table_perm, lax.axis_size(("blk", "grp")), axis=1)),
+                ("blk", "grp"),
+                0,
+                0,
+            ),
+            axis=0,
+        ),
         lax.all_to_all(four_cols, ("blk", "grp"), split_axis=1, concat_axis=0, tiled=True),
     )
     summed = jnp.einsum("rmc,rml->mcl", four_own, table_own, preferred_element_type=jnp.float32)

time: 508 us -> 544 us (1.071); the launches traced: 507 us -> 536 us
  local copies, waits for them, and re-layouts: 90.7 us -> 112 us
  matrix products: 25 us -> 32.7 us
    unnamed x12 -> x43, local copies, waits for them, and re-layouts: 3.99 us -> 56 us
    all_to_all x2 -> x0, local copies, waits for them, and re-layouts: 21.1 us -> none  [per_device(): lax.all_to_all(table_perm, ('blk', 'grp'), split_axis=1, concat_axis=0, t...]
    select_n x1 -> x0, local copies, waits for them, and re-layouts: 12.1 us -> none  [per_device(): table_perm = jnp.take(legendre, owner_table, axis=1)]
    dot_general x1, matrix products: 4.58 us -> 12.3 us  [per_device(): jnp.einsum('rmc,rml->mcl', four_own, table_own, preferred_element_type=jn...]
  transfers between devices with their start and end apart: 3 -> 3, of which waited for: 2 -> 2; matrix products, arithmetic and copies ran while one was open for 11% -> 18% of each run, Pallas kernels for 0% -> 0%
where the time goes in v1:
time: 544 us; the launch traced here: 536 us
  waiting for transfers between devices  318 us (58%)
  local copies, waits for them, and re-layouts  112 us (21%)
  other arithmetic  45.3 us (8%)
  matrix products  32.7 us (6%)
  between operations  14.5 us (3%)
  starting transfers between devices  13.3 us (2%)
    all_to_all x1, waiting for transfers between devices, per_device(): lax.all_to_all(jnp.stack(jnp.split(table_perm, lax.axis_size(('blk', 'grp...  185 us
    unnamed x2, waiting for transfers between devices  134 us
    unnamed x43, local copies, waits for them, and re-layouts  56 us
    gather x1, local copies, waits for them, and re-layouts, per_device(): table_perm = jnp.take(legendre, owner_table, axis=1)  35.4 us
    neg x1, other arithmetic, cycle_fourier(): -jnp.sin(phase)  34.6 us
    dot_general x1, matrix products, cycle_fourier(): jnp.dot(flat, table, precision=lax.Precision.HIGHEST, preferred_element_t...  12.7 us
    dot_general x1, matrix products, per_device(): jnp.einsum('rmc,rml->mcl', four_own, table_own, preferred_element_type=jn...  12.3 us
  transfers between devices with their start and end apart: 3, of which 2 were waited for; matrix products, arithmetic and copies ran while one was open for 18% of the time, Pallas kernels for 0%

profile of v1, /device:TPU:0, one launch (start us, length us, event | category | flops | bytes accessed | tf_op | source)
XLA Modules:
  0.0 535.7 jit_solution(10152660609685607328)
XLA Ops:
  7.2 34.6 %sine_negate_fusion = (f32[4096,512]{1,0:T(8,128)}, f32[4096,512]{1,0:T(8,128)}) fusion(), kind=kLoop, calls=%fused_computation.17 | loop fusion | flops 31457280 | bytes 16777216 | tf_op jit(solution)/shard_map/neg | solution.py:16
  42.0 12.7 %fusion.17 = bf16[16,1024]{1,0:T(8,128)(2,1)S(1)} fusion(f32[16,4096]{1,0:T(8,128)S(1)} %reshape.50, f32[4096,512]{1,0:T(8,128)} %get-tuple-element.4, f32[4096,512]{1,0:T(8,128)} %get-tuple-element.5), kind=kOutput, calls=%fused_computation.25 | convolution fusion | flops 813711360 | bytes 17072128 | tf_op jit(solution)/shard_map/dot_general | solution.py:18
  55.0 2.1 gather_fusion
  57.1 1.8 fusion.52
  60.0 7.3 %all-to-all-start = ((bf16[32,2,256]{2,1,0:T(2,128)(2,1)}), bf16[32,2,256]{2,1,0:T(2,128)(2,1)S(1)}, u32[]{:S(2)}, u32[]{:S(2)}) async-start(bf16[32,2,256]{2,1,0:T(2,128)(2,1)} %reshape.80), calls=%async_computation | async-start | bytes 65536 | tf_op jit(solution)/shard_map/all_to_all | solution.py:50
  67.4 35.4 %gather_fusion.1 = bf16[512,4,2048]{2,0,1:T(8,128)(2,1)} fusion(bf16[4,512,2048]{2,1,0:T(8,128)(2,1)} %param.8, s32[1024]{0:T(1024)S(1)} %pad_clamp_fusion), kind=kCustom, calls=%fused_computation.1 | custom fusion | bytes 16779264 | tf_op jit(solution)/shard_map/jit(_take)/gather | solution.py:37
  102.8 7.6 %select_bitcast_fusion = bf16[4,512,2048]{2,1,0:T(8,128)(2,1)} fusion(bf16[512,4,2048]{2,0,1:T(8,128)(2,1)} %gather_fusion.1, pred[512]{0:T(512)(128)(4,1)S(1)} %compare_and_fusion), kind=kLoop, calls=%fused_computation.15 | loop fusion | flops 4194304 | bytes 16777728 | tf_op jit(solution)/shard_map/jit(_take)/select_n | solution.py:37
  110.3 1.7 fusion.49
  112.1 1.7 fusion.48
  113.7 1.7 fusion.47
  115.4 1.7 fusion.46
  117.1 1.7 fusion.45
  118.8 1.7 fusion.44
  120.4 1.7 fusion.43
  122.1 1.7 fusion.42
  123.8 1.7 fusion.41
  125.5 1.7 fusion.40
  127.1 1.7 fusion.39
  128.8 1.7 fusion.38
  130.5 1.7 fusion.37
  132.2 1.7 fusion.36
  133.8 1.7 fusion.35
  135.5 1.7 fusion.34
  137.2 1.7 fusion.33
  138.8 1.7 fusion.32
  140.5 1.7 fusion.31
  142.2 1.7 fusion.30
  143.9 1.7 fusion.29
  145.5 1.7 fusion.28
  147.2 1.7 fusion.27
  148.9 1.7 fusion.26
  150.6 1.7 fusion.25
  152.3 1.7 fusion.24
  153.9 1.7 fusion.23
  155.6 1.7 fusion.22
  157.3 1.7 fusion.21
  159.0 1.7 fusion.20
  160.7 1.7 fusion.19
  162.3 1.7 fusion.18
  164.0 6.0 %all-to-all-start.1 = ((bf16[32,4,16,2048]{3,2,1,0:T(8,128)(2,1)}), bf16[32,4,16,2048]{3,2,1,0:T(8,128)(2,1)}, u32[]{:S(2)}, u32[]{:S(2)}) async-start(bf16[32,4,16,2048]{3,2,1,0:T(8,128)(2,1)} %fusion.18), calls=%async_computation.1 | async-start | bytes 16777216 | tf_op jit(solution)/shard_map/all_to_all | solution.py:42
  171.3 184.5 %all-to-all-done.1 = bf16[32,4,16,2048]{3,2,1,0:T(8,128)(2,1)} async-done(((bf16[32,4,16,2048]{3,2,1,0:T(8,128)(2,1)}), bf16[32,4,16,2048]{3,2,1,0:T(8,128)(2,1)}, u32[]{:S(2)}, u32[]{:S(2)}) %all-to-all-start.1) | async-done | bytes 8388640 | tf_op jit(solution)/shard_map/all_to_all | solution.py:42
  355.9 12.3 %fusion.13 = f32[16,8,2048]{2,1,0:T(8,128)S(1)} fusion(bf16[128,16,8]{0,2,1:T(8,128)(2,1)S(1)} %copy.27, bf16[128,16,2048]{2,1,0:T(8,128)(2,1)} %bitcast.41, pred[16,2048]{1,0:T(8,128)(4,1)S(1)} %iota_compare_fusion), kind=kOutput, calls=%fused_computation.22 | convolution fusion | flops 67371008 | bytes 9502720 | tf_op jit(solution)/shard_map/rmc,rml->mcl/dot_general | solution.py:52
  368.8 5.7 %copy.29 = bf16[16,4,2,2048]{0,1,2,3:T(4,128)(2,1)} copy(f32[16,4,2,2048]{3,2,1,0:T(2,128)S(1)} %reshape.52) | data formatting | bytes 1572864 | tf_op jit(solution)/shard_map/reshape | solution.py:56
  375.0 4.9 copy.28
  380.0 7.8 %convolution_bitcast_fusion = f32[4,4,2048]{1,0,2:T(4,128)} fusion(bf16[16,4,2,2048]{0,1,2,3:T(4,128)(2,1)} %copy.28, bf16[16,4,2,2048]{0,1,2,3:T(4,128)(2,1)} %copy.29), kind=kOutput, calls=%fused_computation.23 | convolution fusion | flops 2097152 | bytes 1179648 | tf_op jit(solution)/shard_map/m,miql,mjql->ijl/dot_general | solution.py:58
  387.7 3.6 copy.30
  392.1 1.3 copy.35
  393.4 133.7 %reduce-scatter.4.cloned.1.call-done = f32[64,10]{1,0:T(8,128)} async-done(((f32[2048,10]{1,0:T(8,128)}), f32[64,10]{1,0:T(8,128)}) %reduce-scatter.4.cloned.1.call-update) | async-done | bytes 2576
  (30 shorter events, 6.4 us)
Async XLA Ops:
  7.2 34.6 %copy-start.3 = (s32[512]{0:T(512)S(1)}, s32[512]{0:T(512)}, u32[]{:S(2)}) copy-start(s32[512]{0:T(512)} %param.9) | copy-start | bytes 6148
  7.2 34.7 %copy-start.1 = (f32[4,4,4096]{2,1,0:T(4,128)S(1)}, f32[4,4,4096]{2,1,0:T(4,128)}, u32[]{:S(2)}) copy-start(f32[4,4,4096]{2,1,0:T(4,128)} %param.7) | copy-start | bytes 786436
  60.0 104.0 %all-to-all-start = ((bf16[32,2,256]{2,1,0:T(2,128)(2,1)}), bf16[32,2,256]{2,1,0:T(2,128)(2,1)S(1)}, u32[]{:S(2)}, u32[]{:S(2)}) async-start(bf16[32,2,256]{2,1,0:T(2,128)(2,1)} %reshape.80), calls=%async_computation | async-start | bytes 65536 | tf_op jit(solution)/shard_map/all_to_all | solution.py:50
  164.0 191.9 %all-to-all-start.1 = ((bf16[32,4,16,2048]{3,2,1,0:T(8,128)(2,1)}), bf16[32,4,16,2048]{3,2,1,0:T(8,128)(2,1)}, u32[]{:S(2)}, u32[]{:S(2)}) async-start(bf16[32,4,16,2048]{3,2,1,0:T(8,128)(2,1)} %fusion.18), calls=%async_computation.1 | async-start | bytes 16777216 | tf_op jit(solution)/shard_map/all_to_all | solution.py:42
  170.0 357.2 %reduce-scatter.4.cloned.1.call-start = ((), (), s32[]{:S(2)}) async-start(), calls=%async_computation.3 | async-start | bytes 1081344
  368.8 18.9 %copy-start = (f32[16,4,2,2048]{3,2,1,0:T(2,128)}, f32[16,4,2,2048]{3,2,1,0:T(2,128)S(1)}, u32[]{:S(2)}) copy-start(f32[16,4,2,2048]{3,2,1,0:T(2,128)S(1)} %reshape.52) | copy-start | bytes 3145732
  380.0 11.3 %copy-start.2 = (s32[10]{0:T(128)S(1)}, s32[10]{0:T(128)}, u32[]{:S(2)}) copy-start(s32[10]{0:T(128)} %constant.109) | copy-start | bytes 124
Sparse Core Ops, SparseCore 0:
  393.5 133.5 reduce-scatter.3
